TPU v7x, 256 devices: a whole 4x4x8 slice. The times are simulated.
256 devices in a mesh: dp: 8 (over z), mp: 32 (over x, y, core).
Axes of the slice: x: 4, y: 4, z: 8, core: 2. Of those that a mesh axis runs over, the one named last changes fastest.
Arguments:
- activations: bfloat16 [12288, 8192], P('dp', 'mp'), may hold values from -6 to 6
- grad_output: bfloat16 [12288, 16384], P('dp', 'mp'), may hold values from -0.0546875 to 0.0546875
- holder_index: int32 [32, 32, 1], replicated, may hold values from 0 to 31; in each aligned block of 32 rows (0 to 31, 32 to 63, ..., all dimensions but the last counted through in order) no two rows name the same one
- row_offset: int32 [32, 32], replicated, may hold values from 0 to 1
- column_offset: int32 [32, 32], replicated, may hold values from 0 to 3
- live_counts: int32 [32], replicated, may hold values from 1 to 32, as said below
Outputs:
- candidate_grads: float32 [32, 32, 128, 128], P('mp', 'dp')
Inputs may be any that keep to these rules, and one draw needn't show every extreme that they name: In each owner's 32 slots at most 1 have the same holder_index, a bound that some block reaches. Slots from live_counts[o] on are unused; some owner uses all 32 slots.
All inputs are finite; a program needn't handle non-finite values.
Results may differ from a plain program's by a relative error of at most 0.0003.
Values may be sent and summed in bfloat16 or wider, within the bound.
A program may use at most 192 MiB of HBM per device.

v0:
```python
import jax
import jax.numpy as jnp
from jax import lax
from jax.sharding import PartitionSpec as P

BLK = 128


def on_device(activations, grad_output, holder_index, row_offset, column_offset, live_counts):
    owners = lax.axis_size("mp")
    my_index = lax.axis_index("mp")
    tokens_here = activations.shape[0]
    block_size = BLK
    per_holder = activations.shape[1] // block_size
    per_owner = grad_output.shape[1] // block_size
    slot_count = row_offset.shape[1]
    holders_all = holder_index[:, :, 0]
    my_holder = lax.dynamic_index_in_dim(holders_all, my_index, 0, keepdims=False)
    my_offset = lax.dynamic_index_in_dim(row_offset, my_index, 0, keepdims=False)
    my_column = lax.dynamic_index_in_dim(column_offset, my_index, 0, keepdims=False)
    my_count = lax.dynamic_index_in_dim(live_counts, my_index, 0, keepdims=False)
    grad_panels = grad_output.reshape(tokens_here, per_owner, block_size)
    is_used = jnp.arange(slot_count, dtype=jnp.int32) < my_count
    gathered = lax.all_gather(activations, "mp", axis=1, tiled=True)
    input_panels = gathered.reshape(tokens_here, owners * per_holder, block_size)
    picked_input = jnp.take(input_panels, my_holder * per_holder + my_offset, axis=1)
    picked_grad = jnp.take(grad_panels, my_column, axis=1)
    blocks = jnp.einsum(
        "tkr,tkc->krc", picked_input, picked_grad, preferred_element_type=jnp.float32
    )
    blocks = jnp.where(is_used[:, None, None], blocks, jnp.zeros_like(blocks))
    summed = lax.psum_scatter(blocks, "dp", scatter_dimension=0, tiled=True)
    return summed[None]


def solution(mesh):
    placed = (P("dp", "mp"), P("dp", "mp"), P(), P(), P(), P())
    return jax.shard_map(
        on_device, mesh=mesh, in_specs=placed, out_specs=P("mp", "dp", None, None), check_vma=False
    )
```

profile of v0, /device:TPU:8, one launch (start us, length us, event | category | flops | bytes accessed | tf_op | source)
XLA Modules:
  0.0 218.2 jit_solution(10876988246846555151)
XLA Ops:
  6.5 0.0 all-gather.2.cloned.1.call-start
  6.5 2.3 %copy.9 = bf16[1536,256]{0,1:T(8,128)(2,1)} copy(bf16[1536,256]{1,0:T(8,128)(2,1)} %param.6) | data formatting | bytes 1572864 | tf_op args[0]
  8.9 0.0 all-gather.2.cloned.1.call-update
  8.9 0.0 reduce-scatter.2.cloned.1.call-start
  9.0 1.7 copy.11
  10.7 0.9 copy.12
  11.6 1.2 dynamic_slice.14
  12.8 0.7 fusion.15
  13.5 6.6 %gather_fusion.1 = bf16[32,1536,128]{2,1,0:T(8,128)(2,1)} fusion(bf16[1536,4,128]{2,0,1:T(8,128)(2,1)S(1)} %copy.12, s32[1024]{0:T(1024)S(1)} %pad_clamp_fusion), kind=kCustom, calls=%fused_computation.1 | custom fusion | bytes 25165952 | tf_op jit(solution)/shard_map/jit(_take)/gather | solution.py:27
  20.1 0.6 iota_compare_fusion
  20.7 0.7 fusion.14
  21.4 0.7 compare_and_fusion
  22.2 86.9 %all-gather.2.cloned.1.call-done = bf16[1536,8192]{0,1:T(8,128)(2,1)} async-done(((bf16[1536,256]{0,1:T(8,128)(2,1)}), bf16[1536,8192]{0,1:T(8,128)(2,1)}) %all-gather.2.cloned.1.call-update) | async-done | bytes 25165840 | tf_op jit(solution)/shard_map/all_gather | solution.py:24
  109.1 32.4 %copy.10 = bf16[1536,64,128]{2,0,1:T(8,128)(2,1)} copy(bf16[1536,64,128]{0,2,1:T(8,128)(2,1)} %bitcast.34) | data formatting | bytes 50331648 | tf_op jit(solution)/shard_map/reshape | solution.py:25
  141.5 14.9 %gather_fusion = bf16[32,1536,128]{2,1,0:T(8,128)(2,1)} fusion(bf16[1536,64,128]{2,0,1:T(8,128)(2,1)} %copy.10, s32[1024]{0:T(1024)S(1)} %pad_clamp_fusion.1), kind=kCustom, calls=%fused_computation | custom fusion | bytes 25165952 | tf_op jit(solution)/shard_map/jit(_take)/gather | solution.py:26
  156.4 11.9 %fusion.8 = f32[32,128,128]{2,1,0:T(8,128)} fusion(bf16[32,1536,128]{2,1,0:T(8,128)(2,1)} %gather_fusion.1, pred[32]{0:T(512)(128)(4,1)S(1)} %get-tuple-element.5, bf16[32,1536,128]{2,1,0:T(8,128)(2,1)} %gather_fusion, pred[32]{0:T(512)(128)(4,1)S(1)} %get-tuple-element.6, pred[32]{0:T(512)(128)(4,1)S(1)} %iota_compare_fusion), kind=kOutput, calls=%fused_computation.10 | convolution fusion | flops 1623719936 | bytes 27263072 | tf_op jit(solution)/shard_map/tkr,tkc->krc/dot_general | solution.py:28
  168.4 0.0 reduce-scatter.2.cloned.1.call-update
  168.4 43.0 %reduce-scatter.2.cloned.1.call-done = f32[4,128,128]{2,1,0:T(8,128)} async-done(((f32[32,128,128]{2,1,0:T(8,128)}), f32[4,128,128]{2,1,0:T(8,128)}) %reduce-scatter.2.cloned.1.call-update) | async-done | bytes 262160 | tf_op jit(solution)/shard_map/reduce_scatter | solution.py:32
  (2 shorter events, 0.0 us)
Async XLA Ops:
  6.5 102.6 %all-gather.2.cloned.1.call-start = ((), (), s32[]{:S(2)}) async-start(), calls=%async_computation.1 | async-start | bytes 25952256 | tf_op jit(solution)/shard_map/all_gather | solution.py:24
  8.9 202.5 %reduce-scatter.2.cloned.1.call-start = ((), (), s32[]{:S(2)}) async-start(), calls=%async_computation.2 | async-start | bytes 2359296 | tf_op jit(solution)/shard_map/reduce_scatter | solution.py:32
Sparse Core Ops, SparseCore 0:
  9.9 99.1 all-gather.1
  168.5 42.8 reduce-scatter.1
where the time goes:
time: 219 us; the launch traced here: 218 us
  waiting for transfers between devices  130 us (59%)
  local copies, waits for them, and re-layouts  60.1 us (27%)
  between operations  13.4 us (6%)
  matrix products  11.9 us (5%)
  other arithmetic  2.77 us (1%)
    all_gather x1, waiting for transfers between devices, on_device(): gathered = lax.all_gather(activations, 'mp', axis=1, tiled=True)  86.9 us
    reduce_scatter x1, waiting for transfers between devices, on_device(): summed = lax.psum_scatter(blocks, 'dp', scatter_dimension=0, tiled=True)  43 us
    reshape x1, local copies, waits for them, and re-layouts, on_device(): gathered.reshape(tokens_here, owners * per_holder, block_size)  32.4 us
    gather x1, local copies, waits for them, and re-layouts, on_device(): jnp.take(input_panels, my_holder * per_holder + my_offset, axis=1)  14.9 us
    dot_general x1, matrix products, on_device(): jnp.einsum('tkr,tkc->krc', picked_input, picked_grad, preferred_element_t...  11.9 us
    gather x1, local copies, waits for them, and re-layouts, on_device(): picked_grad = jnp.take(grad_panels, my_column, axis=1)  6.55 us
  transfers between devices with their start and end apart: 2, of which 2 were waited for; matrix products, arithmetic and copies ran while one was open for 6% of the time, Pallas kernels for 0%

commit v1 on v0

--- a/solution.py
+++ b/solution.py
@@ -4,6 +4,11 @@
 from jax.sharding import PartitionSpec as P
 
 BLK = 128
+
+
+def gather_by_exchange(x, axis, dim):
+    copies = jnp.concatenate([x] * lax.axis_size(axis), axis=dim)
+    return lax.all_to_all(copies, axis, dim, dim, tiled=True)
 
 
 def on_device(activations, grad_output, holder_index, row_offset, column_offset, live_counts):
@@ -21,7 +26,7 @@
     my_count = lax.dynamic_index_in_dim(live_counts, my_index, 0, keepdims=False)
     grad_panels = grad_output.reshape(tokens_here, per_owner, block_size)
     is_used = jnp.arange(slot_count, dtype=jnp.int32) < my_count
-    gathered = lax.all_gather(activations, "mp", axis=1, tiled=True)
+    gathered = gather_by_exchange(activations, "mp", 1)
     input_panels = gathered.reshape(tokens_here, owners * per_holder, block_size)
     picked_input = jnp.take(input_panels, my_holder * per_holder + my_offset, axis=1)
     picked_grad = jnp.take(grad_panels, my_column, axis=1)

time: 219 us -> 620 us (2.83)
  waiting for transfers between devices: 130 us -> 443 us
  local copies, waits for them, and re-layouts: 60.1 us -> 138 us
  starting transfers between devices: 0.04 us -> 7.76 us
    all_to_all x0 -> x1, waiting for transfers between devices: none -> 398 us  [gather_by_exchange(): return lax.all_to_all(copies, axis, dim, dim, tiled=True)]
    all_gather x1 -> x0, waiting for transfers between devices: 86.9 us -> none  [on_device(): gathered = lax.all_gather(activations, 'mp', axis=1, tiled=True)]
    unnamed x2 -> x38, local copies, waits for them, and re-layouts: 4.06 us -> 49 us
    concatenate x0 -> x2, local copies, waits for them, and re-layouts: none -> 33.6 us  [gather_by_exchange(): copies = jnp.concatenate([x] * lax.axis_size(axis), axis=dim)]
    all_to_all x0 -> x1, starting transfers between devices: none -> 7.72 us  [gather_by_exchange(): return lax.all_to_all(copies, axis, dim, dim, tiled=True)]
  transfers between devices with their start and end apart: 2 -> 2, of which waited for: 2 -> 2; matrix products, arithmetic and copies ran while one was open for 6% -> 2% of each run, Pallas kernels for 0% -> 0%
where the time goes in v1:
time: 620 us; the launch traced here: 617 us
  waiting for transfers between devices  443 us (71%)
  local copies, waits for them, and re-layouts  138 us (22%)
  between operations  13.5 us (2%)
  matrix products  12 us (2%)
  starting transfers between devices  7.76 us (1%)
    all_to_all x1, waiting for transfers between devices, gather_by_exchange(): return lax.all_to_all(copies, axis, dim, dim, tiled=True)  398 us
    unnamed x38, local copies, waits for them, and re-layouts  49 us
    reduce_scatter x1, waiting for transfers between devices, on_device(): summed = lax.psum_scatter(blocks, 'dp', scatter_dimension=0, tiled=True)  45.2 us
    concatenate x2, local copies, waits for them, and re-layouts, gather_by_exchange(): copies = jnp.concatenate([x] * lax.axis_size(axis), axis=dim)  33.6 us
    reshape x1, local copies, waits for them, and re-layouts, on_device(): gathered.reshape(tokens_here, owners * per_holder, block_size)  32.5 us
    gather x1, local copies, waits for them, and re-layouts, on_device(): jnp.take(input_panels, my_holder * per_holder + my_offset, axis=1)  14.9 us
  transfers between devices with their start and end apart: 2, of which 2 were waited for; matrix products, arithmetic and copies ran while one was open for 2% of the time, Pallas kernels for 0%

profile of v1, /device:TPU:8, one launch (start us, length us, event | category | flops | bytes accessed | tf_op | source)
XLA Modules:
  0.0 617.1 jit_solution(2192591255715202992)
XLA Ops:
  6.5 2.2 constant_dynamic-update-slice_fusion.31
  8.7 2.1 constant_dynamic-update-slice_fusion.30
  10.8 2.1 constant_dynamic-update-slice_fusion.29
  12.9 2.1 constant_dynamic-update-slice_fusion.28
  15.1 2.1 constant_dynamic-update-slice_fusion.27
  17.2 2.1 constant_dynamic-update-slice_fusion.26
  19.3 2.1 constant_dynamic-update-slice_fusion.25
  21.4 2.1 constant_dynamic-update-slice_fusion.24
  23.5 2.1 constant_dynamic-update-slice_fusion.23
  25.6 2.1 constant_dynamic-update-slice_fusion.22
  27.7 2.1 constant_dynamic-update-slice_fusion.21
  29.8 2.1 constant_dynamic-update-slice_fusion.20
  31.9 2.1 constant_dynamic-update-slice_fusion.19
  34.0 2.1 constant_dynamic-update-slice_fusion.18
  36.1 2.1 constant_dynamic-update-slice_fusion.17
  38.2 2.1 constant_dynamic-update-slice_fusion.16
  40.3 0.9 constant_dynamic-update-slice_fusion.15
  41.2 0.9 constant_dynamic-update-slice_fusion.14
  42.2 1.0 constant_dynamic-update-slice_fusion.13
  43.1 1.0 constant_dynamic-update-slice_fusion.12
  44.1 1.0 constant_dynamic-update-slice_fusion.11
  45.1 1.0 constant_dynamic-update-slice_fusion.10
  46.1 0.9 constant_dynamic-update-slice_fusion.9
  47.0 0.9 constant_dynamic-update-slice_fusion.8
  48.0 1.0 constant_dynamic-update-slice_fusion.7
  48.9 1.0 constant_dynamic-update-slice_fusion.6
  49.9 1.0 constant_dynamic-update-slice_fusion.5
  50.9 0.9 constant_dynamic-update-slice_fusion.4
  51.9 1.0 constant_dynamic-update-slice_fusion.3
  52.8 1.0 constant_dynamic-update-slice_fusion.2
  53.8 1.0 constant_dynamic-update-slice_fusion.1
  54.8 1.0 constant_dynamic-update-slice_fusion
  55.8 32.6 %copy.9 = bf16[1536,8192]{0,1:T(8,128)(2,1)} copy(bf16[1536,8192]{1,0:T(8,128)(2,1)} %constant_dynamic-update-slice_fusion) | data formatting | bytes 50331648 | tf_op jit(solution)/shard_map/concatenate | solution.py:10
  88.4 7.7 %all-to-all-start = ((bf16[1536,32,256]{0,2,1:T(8,128)(2,1)}), bf16[1536,32,256]{0,2,1:T(8,128)(2,1)}, u32[]{:S(2)}, u32[]{:S(2)}) async-start(bf16[1536,32,256]{0,2,1:T(8,128)(2,1)} %bitcast.35), calls=%async_computation | async-start | bytes 50331648 | tf_op jit(solution)/shard_map/all_to_all | solution.py:11
  96.1 0.0 reduce-scatter.2.cloned.1.call-start
  96.2 0.7 copy.11
  96.9 0.9 copy.12
  97.8 0.6 dynamic_slice.14
  98.4 0.7 fusion.15
  99.1 0.7 fusion.14
  99.8 6.5 %gather_fusion.1 = bf16[32,1536,128]{2,1,0:T(8,128)(2,1)} fusion(bf16[1536,4,128]{2,0,1:T(8,128)(2,1)S(1)} %copy.12, s32[1024]{0:T(1024)S(1)} %get-tuple-element.7), kind=kCustom, calls=%fused_computation.1 | custom fusion | bytes 25165952 | tf_op jit(solution)/shard_map/jit(_take)/gather | solution.py:32
  106.3 0.6 iota_compare_fusion
  107.0 0.7 compare_and_fusion
  107.7 397.9 %all-to-all-done = bf16[1536,32,256]{0,2,1:T(8,128)(2,1)} async-done(((bf16[1536,32,256]{0,2,1:T(8,128)(2,1)}), bf16[1536,32,256]{0,2,1:T(8,128)(2,1)}, u32[]{:S(2)}, u32[]{:S(2)}) %all-to-all-start) | async-done | bytes 25165856 | tf_op jit(solution)/shard_map/all_to_all | solution.py:11
  505.6 32.5 %copy.10 = bf16[1536,64,128]{2,0,1:T(8,128)(2,1)} copy(bf16[1536,64,128]{0,2,1:T(8,128)(2,1)} %bitcast.4) | data formatting | bytes 50331648 | tf_op jit(solution)/shard_map/reshape | solution.py:30
  538.1 14.9 %gather_fusion = bf16[32,1536,128]{2,1,0:T(8,128)(2,1)} fusion(bf16[1536,64,128]{2,0,1:T(8,128)(2,1)} %copy.10, s32[1024]{0:T(1024)S(1)} %get-tuple-element.8), kind=kCustom, calls=%fused_computation | custom fusion | bytes 25165952 | tf_op jit(solution)/shard_map/jit(_take)/gather | solution.py:31
  553.0 12.0 %fusion.8 = f32[32,128,128]{2,1,0:T(8,128)} fusion(bf16[32,1536,128]{2,1,0:T(8,128)(2,1)} %gather_fusion.1, pred[32]{0:T(512)(128)(4,1)S(1)} %get-tuple-element.5, bf16[32,1536,128]{2,1,0:T(8,128)(2,1)} %gather_fusion, pred[32]{0:T(512)(128)(4,1)S(1)} %get-tuple-element.6, pred[32]{0:T(512)(128)(4,1)S(1)} %iota_compare_fusion), kind=kOutput, calls=%fused_computation.10 | convolution fusion | flops 1623719936 | bytes 27263072 | tf_op jit(solution)/shard_map/tkr,tkc->krc/dot_general | solution.py:33
  565.0 45.2 %reduce-scatter.2.cloned.1.call-done = f32[4,128,128]{2,1,0:T(8,128)} async-done(((f32[32,128,128]{2,1,0:T(8,128)}), f32[4,128,128]{2,1,0:T(8,128)}) %reduce-scatter.2.cloned.1.call-update) | async-done | bytes 262160 | tf_op jit(solution)/shard_map/reduce_scatter | solution.py:37
  (8 shorter events, 0.0 us)
Async XLA Ops:
  6.5 33.7 %copy-start = (bf16[1536,256]{1,0:T(8,128)(2,1)S(1)}, bf16[1536,256]{1,0:T(8,128)(2,1)}, u32[]{:S(2)}) copy-start(bf16[1536,256]{1,0:T(8,128)(2,1)} %param.6) | copy-start | bytes 2359300
  88.4 7.8 %copy-start.1 = (bf16[1536,512]{1,0:T(8,128)(2,1)S(1)}, bf16[1536,512]{1,0:T(8,128)(2,1)}, u32[]{:S(2)}) copy-start(bf16[1536,512]{1,0:T(8,128)(2,1)} %param.7) | copy-start | bytes 4718596
  88.4 9.4 %copy-start.2 = (s32[32]{0:T(128)S(1)}, s32[32]{0:T(128)}, u32[]{:S(2)}) copy-start(s32[32]{0:T(128)} %param.11) | copy-start | bytes 388
  88.4 417.2 %all-to-all-start = ((bf16[1536,32,256]{0,2,1:T(8,128)(2,1)}), bf16[1536,32,256]{0,2,1:T(8,128)(2,1)}, u32[]{:S(2)}, u32[]{:S(2)}) async-start(bf16[1536,32,256]{0,2,1:T(8,128)(2,1)} %bitcast.35), calls=%async_computation | async-start | bytes 50331648 | tf_op jit(solution)/shard_map/all_to_all | solution.py:11
  96.1 514.1 %reduce-scatter.2.cloned.1.call-start = ((), (), s32[]{:S(2)}) async-start(), calls=%async_computation.2 | async-start | bytes 2359296 | tf_op jit(solution)/shard_map/reduce_scatter | solution.py:37
Sparse Core Ops, SparseCore 0:
  565.1 45.0 reduce-scatter.1
